TPU v7x, 256 devices: a whole 4x4x8 slice. The times are simulated.
256 devices in a mesh: dp: 8 (over x, core), expert: 32 (over z, y).
Axes of the slice: x: 4, y: 4, z: 8, core: 2. Of those that a mesh axis runs over, the one named last changes fastest.
Arguments:
- tokens: bfloat16 [32768, 1024], P(('dp', 'expert')), may hold values from -6 to 6
- route_a: int32 [32768, 1], P(('dp', 'expert')), may hold values from 0 to 31
- route_b: int32 [32768, 1], P(('dp', 'expert')), may hold values from 0 to 63
- gain_a: float32 [1024], replicated, may hold values from 0.25 to 1.75
- gain_b: float32 [1024], replicated, may hold values from 0.25 to 1.75
- router_a: bfloat16 [1024, 32], replicated, may hold values from -0.375 to 0.375
- router_b: bfloat16 [1024, 64], replicated, may hold values from -0.375 to 0.375
- dense_in_a: bfloat16 [1024, 4096], P(None, 'dp'), may hold values from -0.1875 to 0.1875
- dense_out_a: bfloat16 [4096, 1024], P('dp'), may hold values from -0.09375 to 0.09375
- dense_in_b: bfloat16 [1024, 4096], P(None, 'dp'), may hold values from -0.1875 to 0.1875
- dense_out_b: bfloat16 [4096, 1024], P('dp'), may hold values from -0.09375 to 0.09375
- expert_in_a: bfloat16 [32, 1024, 4096], P('expert', None, 'dp'), may hold values from -0.1875 to 0.1875
- expert_out_a: bfloat16 [32, 4096, 1024], P('expert', 'dp'), may hold values from -0.09375 to 0.09375
- expert_in_b: bfloat16 [64, 1024, 4096], P('expert', None, 'dp'), may hold values from -0.1875 to 0.1875
- expert_out_b: bfloat16 [64, 4096, 1024], P('expert', 'dp'), may hold values from -0.09375 to 0.09375
Outputs:
- stream_out: bfloat16 [32768, 1024], P(('dp', 'expert'))
All inputs are finite; a program needn't handle non-finite values.
Results may differ from a plain program's by a relative error of at most 0.0091.
Values may be sent and summed in bfloat16 or wider, within the bound.
A program may use at most 128 MiB of HBM per device.

v0:
```python
import jax
import jax.numpy as jnp
from jax import lax
from jax.sharding import PartitionSpec as P


def in_order(blocks, dim):
    shape = list(blocks.shape[1:])
    shape[dim] *= blocks.shape[0]
    return jnp.moveaxis(blocks, 0, dim).reshape(shape)


def from_everyone(value, axis):
    copies = jnp.broadcast_to(value, (lax.axis_size(axis), *value.shape))
    return lax.all_to_all(copies, axis, split_axis=0, concat_axis=0, tiled=True)


def gather_directly(value, axis, dim):
    return in_order(from_everyone(value, axis), dim)


def in_blocks(value, dim, devices):
    before, after = (value.shape[:dim], value.shape[dim + 1 :])
    return jnp.moveaxis(value.reshape(*before, devices, -1, *after), dim, 0)


def summed_on_arrival(value, axis, dim):
    devices = lax.axis_size(axis)
    blocks = lax.all_to_all(in_blocks(value, dim, devices), axis, 0, 0, tiled=True)
    return jnp.sum(blocks.astype(jnp.float32), axis=0)


def norm_rows(x, gain):
    xf = x.astype(jnp.float32)
    mean = jnp.mean(xf, axis=-1, keepdims=True)
    var = jnp.mean((xf - mean) ** 2, axis=-1, keepdims=True)
    return ((xf - mean) / jnp.sqrt(var + 1e-05) * gain).astype(jnp.bfloat16)


def rank_table(blocks, experts):
    onehot = (blocks[:, :, None] == jnp.arange(experts)[None, None, :]).astype(jnp.int32)
    before = jnp.cumsum(onehot, axis=1) - onehot
    rank = jnp.sum(before * onehot, axis=-1)
    return (onehot, rank)


def moe_layer(x, ids, gain, router, d_in, d_out, e_in, e_out):
    tok_rows, width = x.shape
    experts = router.shape[1]
    owners = lax.axis_size("expert")
    per_dev = experts // owners
    cap = (5 * tok_rows + 4 * experts - 1) // (4 * experts)
    normed = norm_rows(x, gain)
    onehot, rank = rank_table(ids.reshape(1, tok_rows), experts)
    rank = rank.reshape(-1)
    kept = rank < cap
    total = experts * cap
    slot_row = jnp.where(kept, ids * cap + rank, total)
    logits = jnp.dot(normed, router, preferred_element_type=jnp.float32)
    picked = jnp.sum(logits * onehot.reshape(-1, experts).astype(jnp.float32), axis=-1)
    gate = jax.nn.sigmoid(picked) * kept.astype(jnp.float32)
    dense_act = jax.nn.gelu(
        jnp.dot(gather_directly(normed, "dp", 0), d_in, preferred_element_type=jnp.float32),
        approximate=True,
    ).astype(jnp.bfloat16)
    rows = dense_act
    dense = summed_on_arrival(
        jnp.dot(rows, d_out, preferred_element_type=jnp.float32).astype(jnp.bfloat16), "dp", 0
    )
    buffer = jnp.zeros((total, width), jnp.bfloat16).at[slot_row].set(normed, mode="drop")
    buffer = buffer.reshape(owners, per_dev, cap, width)
    arrived = lax.all_to_all(buffer, "expert", split_axis=0, concat_axis=0, tiled=True)
    expert_act = jax.nn.gelu(
        jnp.einsum(
            "secd,edf->secf",
            lax.all_gather(arrived, "dp", axis=0, tiled=True),
            e_in,
            preferred_element_type=jnp.float32,
        ),
        approximate=True,
    ).astype(jnp.bfloat16)
    rows = expert_act
    partial_value = lax.psum_scatter(
        jnp.einsum("secf,efd->secd", rows, e_out, preferred_element_type=jnp.float32).astype(
            jnp.bfloat16
        ),
        "dp",
        scatter_dimension=0,
        tiled=True,
    ).astype(jnp.float32)
    returned = (
        lax.all_to_all(
            partial_value.astype(jnp.bfloat16), "expert", split_axis=0, concat_axis=0, tiled=True
        )
        .astype(partial_value.dtype)
        .reshape(total, width)
    )
    expert_tok = jnp.take(returned, slot_row, axis=0, mode="fill", fill_value=0.0)
    return (x.astype(jnp.float32) + dense + gate[:, None] * expert_tok).astype(jnp.bfloat16)


def body(
    tokens,
    route_a,
    route_b,
    gain_a,
    gain_b,
    router_a,
    router_b,
    dense_in_a,
    dense_out_a,
    dense_in_b,
    dense_out_b,
    expert_in_a,
    expert_out_a,
    expert_in_b,
    expert_out_b,
):
    middle = moe_layer(
        tokens, route_a[:, 0], gain_a, router_a, dense_in_a, dense_out_a, expert_in_a, expert_out_a
    )
    return moe_layer(
        middle, route_b[:, 0], gain_b, router_b, dense_in_b, dense_out_b, expert_in_b, expert_out_b
    )


def solution(mesh):
    in_specs = (
        P(("dp", "expert"), None),
        P(("dp", "expert"), None),
        P(("dp", "expert"), None),
        P(),
        P(),
        P(),
        P(),
        P(None, "dp"),
        P("dp", None),
        P(None, "dp"),
        P("dp", None),
        P("expert", None, "dp"),
        P("expert", "dp", None),
        P("expert", None, "dp"),
        P("expert", "dp", None),
    )
    out_specs = P(("dp", "expert"), None)
    return jax.shard_map(body, mesh=mesh, in_specs=in_specs, out_specs=out_specs, check_vma=False)
```

profile of v0, /device:TPU:32, one launch (start us, length us, event | category | flops | bytes accessed | tf_op | source)
XLA Modules:
  0.0 354.0 jit_solution(15019719602853124694)
XLA Ops:
  6.5 0.9 fusion.83
  7.6 0.8 select_reduce_fusion.1
  8.4 0.7 and_bitcast_fusion.1
  9.1 1.1 convert_reduce_fusion.3
  10.2 1.2 fusion.71
  11.4 1.8 scatter_custom_fusion
  13.3 28.4 %all_to_all.40 = bf16[32,1,5,1024]{3,2,1,0:T(8,128)(2,1)S(1)} all-to-all(bf16[32,1,5,1024]{3,2,1,0:T(8,128)(2,1)S(1)} %bitcast.99), channel_id=1, replica_groups=mesh['dp'=8,'expert'=32] {'expert'}, dimensions={0} | all-to-all | bytes 655360 | tf_op jit(solution)/shard_map/all_to_all | solution.py:72
  41.6 0.9 copy.33
  42.6 25.1 %all-gather.3.cloned.1.call-done = bf16[256,1,5,1024]{3,0,2,1:T(8,128)(2,1)} async-done(((bf16[32,1,5,1024]{3,0,2,1:T(8,128)(2,1)}), bf16[256,1,5,1024]{3,0,2,1:T(8,128)(2,1)}) %all-gather.3.cloned.1.call-update) | async-done | bytes 2621456 | tf_op jit(solution)/shard_map/all_gather | solution.py:76
  67.7 7.1 %convert_bitcast_fusion.1 = bf16[256,1,5,1024]{3,0,2,1:T(8,128)(2,1)} fusion(bf16[1,512,1024]{2,1,0:T(8,128)(2,1)} %param.27, bf16[256,1,5,1024]{3,0,2,1:T(8,128)(2,1)} %all-gather.3.cloned.1.call-done, bf16[1,1024,512]{2,1,0:T(8,128)(2,1)} %param.26), kind=kOutput, calls=%fused_computation.29 | convolution fusion | flops 2691563520 | bytes 7340032 | tf_op jit(solution)/shard_map/secf,efd->secd/dot_general | solution.py:84
  74.9 0.9 copy-done.1
  76.0 0.3 broadcast_in_dim.49
  76.2 39.3 %all_to_all.41 = bf16[8,128,1024]{2,1,0:T(8,128)(2,1)} all-to-all(bf16[8,128,1024]{2,1,0:T(8,128)(2,1)S(1)} %broadcast_in_dim.49), channel_id=1, replica_groups=mesh['dp'=8,'expert'=32] {'dp'}, dimensions={0} | all-to-all | bytes 4194304 | tf_op jit(solution)/shard_map/all_to_all | solution.py:15
  115.5 6.2 %convolution_convert_fusion.1 = bf16[1024,1024]{1,0:T(8,128)(2,1)} fusion(bf16[512,1024]{1,0:T(8,128)(2,1)} %param.23, bf16[1024,1024]{1,0:T(8,128)(2,1)} %bitcast.97, bf16[1024,512]{1,0:T(8,128)(2,1)} %param.22), kind=kOutput, calls=%fused_computation.50 | convolution fusion | flops 2153250816 | bytes 6291456 | tf_op jit(solution)/shard_map/dot_general | solution.py:68
  121.7 4.5 %all-to-all-start.1 = ((bf16[8,128,1024]{2,1,0:T(8,128)(2,1)}), bf16[8,128,1024]{2,1,0:T(8,128)(2,1)}, u32[]{:S(2)}, u32[]{:S(2)}) async-start(bf16[8,128,1024]{2,1,0:T(8,128)(2,1)} %bitcast.95), calls=%async_computation.1 | async-start | bytes 4194304 | tf_op jit(solution)/shard_map/all_to_all | solution.py:29
  126.7 0.2 fusion.45
  126.9 2.0 copy.34
  128.9 24.5 %all-to-all-done.1 = bf16[8,128,1024]{2,1,0:T(8,128)(2,1)} async-done(((bf16[8,128,1024]{2,1,0:T(8,128)(2,1)}), bf16[8,128,1024]{2,1,0:T(8,128)(2,1)}, u32[]{:S(2)}, u32[]{:S(2)}) %all-to-all-start.1) | async-done | bytes 2097184 | tf_op jit(solution)/shard_map/all_to_all | solution.py:29
  153.4 10.1 %all-to-all-start.3 = ((bf16[32,1,5,1024]{3,2,1,0:T(8,128)(2,1)}), bf16[32,1,5,1024]{3,2,1,0:T(8,128)(2,1)}, u32[]{:S(2)}, u32[]{:S(2)}) async-start(bf16[32,1,5,1024]{3,2,1,0:T(8,128)(2,1)} %copy.34), calls=%async_computation.4 | async-start | bytes 1048576 | tf_op jit(solution)/shard_map/all_to_all | solution.py:92
  163.6 2.8 convert_reduce_fusion.1
  166.4 14.1 %all-to-all-done.3 = bf16[32,1,5,1024]{3,2,1,0:T(8,128)(2,1)} async-done(((bf16[32,1,5,1024]{3,2,1,0:T(8,128)(2,1)}), bf16[32,1,5,1024]{3,2,1,0:T(8,128)(2,1)}, u32[]{:S(2)}, u32[]{:S(2)}) %all-to-all-start.3) | async-done | bytes 327712 | tf_op jit(solution)/shard_map/all_to_all | solution.py:92
  180.5 1.2 reshape.334
  181.7 1.6 gather_fusion
  183.2 1.4 convert_reduce_fusion.2
  184.7 0.2 fusion.68
  184.9 1.4 scatter_custom_fusion.1
  186.3 0.2 reshape.330
  186.5 0.3 copy.35
  186.9 18.9 %all_to_all.42 = bf16[32,2,3,1024]{3,1,2,0:T(2,128)(2,1)S(1)} all-to-all(bf16[32,2,3,1024]{3,1,2,0:T(2,128)(2,1)S(1)} %copy.35), channel_id=1, replica_groups=mesh['dp'=8,'expert'=32] {'expert'}, dimensions={0} | all-to-all | bytes 786432 | tf_op jit(solution)/shard_map/all_to_all | solution.py:72
  205.7 0.8 copy.36
  206.6 0.2 reduce-scatter.5.cloned.1.call-start
  206.8 24.4 %all-gather.5.cloned.1.call-done = bf16[256,2,3,1024]{3,0,2,1:T(8,128)(2,1)} async-done(((bf16[32,2,3,1024]{3,0,2,1:T(8,128)(2,1)}), bf16[256,2,3,1024]{3,0,2,1:T(8,128)(2,1)}) %all-gather.5.cloned.1.call-update) | async-done | bytes 3145744 | tf_op jit(solution)/shard_map/all_gather | solution.py:76
  231.2 7.9 %convert_bitcast_fusion = bf16[256,2,3,1024]{3,0,2,1:T(8,128)(2,1)} fusion(bf16[2,512,1024]{2,1,0:T(8,128)(2,1)S(1)} %copy-done, bf16[256,2,3,1024]{3,0,2,1:T(8,128)(2,1)} %all-gather.5.cloned.1.call-done, bf16[2,1024,512]{2,1,0:T(8,128)(2,1)} %param.28), kind=kOutput, calls=%fused_computation.16 | convolution fusion | flops 3229876224 | bytes 10485760 | tf_op jit(solution)/shard_map/secf,efd->secd/dot_general | solution.py:84
  239.3 0.3 broadcast_in_dim.54
  239.5 38.7 %all_to_all.43 = bf16[8,128,1024]{2,1,0:T(8,128)(2,1)} all-to-all(bf16[8,128,1024]{2,1,0:T(8,128)(2,1)S(1)} %broadcast_in_dim.54), channel_id=1, replica_groups=mesh['dp'=8,'expert'=32] {'dp'}, dimensions={0} | all-to-all | bytes 4194304 | tf_op jit(solution)/shard_map/all_to_all | solution.py:15
  278.3 6.2 %convolution_convert_fusion = bf16[1024,1024]{1,0:T(8,128)(2,1)} fusion(bf16[512,1024]{1,0:T(8,128)(2,1)} %param.25, bf16[1024,1024]{1,0:T(8,128)(2,1)} %bitcast.98, bf16[1024,512]{1,0:T(8,128)(2,1)} %param.24), kind=kOutput, calls=%fused_computation.49 | convolution fusion | flops 2153250816 | bytes 6291456 | tf_op jit(solution)/shard_map/dot_general | solution.py:68
  284.5 4.5 %all-to-all-start.5 = ((bf16[8,128,1024]{2,1,0:T(8,128)(2,1)}), bf16[8,128,1024]{2,1,0:T(8,128)(2,1)}, u32[]{:S(2)}, u32[]{:S(2)}) async-start(bf16[8,128,1024]{2,1,0:T(8,128)(2,1)} %bitcast.96), calls=%async_computation.6 | async-start | bytes 4194304 | tf_op jit(solution)/shard_map/all_to_all | solution.py:29
  289.0 0.9 reduce-scatter.5.cloned.1.call-done
  289.9 2.1 copy.37
  292.0 24.2 %all-to-all-done.5 = bf16[8,128,1024]{2,1,0:T(8,128)(2,1)} async-done(((bf16[8,128,1024]{2,1,0:T(8,128)(2,1)}), bf16[8,128,1024]{2,1,0:T(8,128)(2,1)}, u32[]{:S(2)}, u32[]{:S(2)}) %all-to-all-start.5) | async-done | bytes 2097184 | tf_op jit(solution)/shard_map/all_to_all | solution.py:29
  316.1 10.1 %all-to-all-start.7 = ((bf16[32,2,3,1024]{3,1,2,0:T(2,128)(2,1)}), bf16[32,2,3,1024]{3,1,2,0:T(2,128)(2,1)S(1)}, u32[]{:S(2)}, u32[]{:S(2)}) async-start(bf16[32,2,3,1024]{3,1,2,0:T(2,128)(2,1)} %copy.37), calls=%async_computation.9 | async-start | bytes 786432 | tf_op jit(solution)/shard_map/all_to_all | solution.py:92
  326.3 0.2 fusion.44
  326.5 2.8 convert_reduce_fusion
  329.3 11.3 %all-to-all-done.7 = bf16[32,2,3,1024]{3,1,2,0:T(2,128)(2,1)S(1)} async-done(((bf16[32,2,3,1024]{3,1,2,0:T(2,128)(2,1)}), bf16[32,2,3,1024]{3,1,2,0:T(2,128)(2,1)S(1)}, u32[]{:S(2)}, u32[]{:S(2)}) %all-to-all-start.7) | async-done | bytes 393248 | tf_op jit(solution)/shard_map/all_to_all | solution.py:92
  340.7 1.5 copy.39
  342.3 1.6 reshape.336
  343.9 1.6 gather_fusion.1
  345.4 2.0 fusion.77
  (40 shorter events, 1.4 us)
Async XLA Ops:
  6.5 224.7 %copy-start = (bf16[2,512,1024]{2,1,0:T(8,128)(2,1)S(1)}, bf16[2,512,1024]{2,1,0:T(8,128)(2,1)}, u32[]{:S(2)}) copy-start(bf16[2,512,1024]{2,1,0:T(8,128)(2,1)} %param.29) | copy-start | bytes 6291460
  6.5 61.2 %all-gather.3.cloned.1.call-start = ((), (), s32[]{:S(2)}) async-start(), calls=%async_computation.10 | async-start | bytes 2949120 | tf_op jit(solution)/shard_map/all_gather | solution.py:76
  42.6 84.3 %reduce-scatter.3.cloned.1.call-start = ((), (), s32[]{:S(2)}) async-start(), calls=%async_computation.11 | async-start | bytes 2949120 | tf_op jit(solution)/shard_map/reduce_scatter | solution.py:83
  74.9 0.9 copy-start.1
  74.9 1.0 copy-start.4
  121.7 4.5 %copy-start.7 = (s32[128,1]{0,1:T(1,128)S(1)}, s32[128,1]{0,1:T(1,128)}, u32[]{:S(2)}) copy-start(s32[128,1]{0,1:T(1,128)} %param.17) | copy-start | bytes 1540
  121.7 5.0 %copy-start.3 = (bf16[1024,32]{0,1:T(8,128)(2,1)S(1)}, bf16[1024,32]{0,1:T(8,128)(2,1)}, u32[]{:S(2)}) copy-start(bf16[1024,32]{0,1:T(8,128)(2,1)} %param.20) | copy-start | bytes 196612
  121.7 5.0 %copy-start.6 = (s32[128,1]{0,1:T(1,128)S(1)}, s32[128,1]{0,1:T(1,128)}, u32[]{:S(2)}) copy-start(s32[128,1]{0,1:T(1,128)} %param.16) | copy-start | bytes 1540
  121.7 31.7 %all-to-all-start.1 = ((bf16[8,128,1024]{2,1,0:T(8,128)(2,1)}), bf16[8,128,1024]{2,1,0:T(8,128)(2,1)}, u32[]{:S(2)}, u32[]{:S(2)}) async-start(bf16[8,128,1024]{2,1,0:T(8,128)(2,1)} %bitcast.95), calls=%async_computation.1 | async-start | bytes 4194304 | tf_op jit(solution)/shard_map/all_to_all | solution.py:29
  153.4 27.1 %all-to-all-start.3 = ((bf16[32,1,5,1024]{3,2,1,0:T(8,128)(2,1)}), bf16[32,1,5,1024]{3,2,1,0:T(8,128)(2,1)}, u32[]{:S(2)}, u32[]{:S(2)}) async-start(bf16[32,1,5,1024]{3,2,1,0:T(8,128)(2,1)} %copy.34), calls=%async_computation.4 | async-start | bytes 1048576 | tf_op jit(solution)/shard_map/all_to_all | solution.py:92
  163.5 67.7 %all-gather.5.cloned.1.call-start = ((), (), s32[]{:S(2)}) async-start(), calls=%async_computation.12 | async-start | bytes 3538944 | tf_op jit(solution)/shard_map/all_gather | solution.py:76
  181.6 3.3 copy-start.5
  206.6 83.3 %reduce-scatter.5.cloned.1.call-start = ((), (), s32[]{:S(2)}) async-start(), calls=%async_computation.13 | async-start | bytes 3538944 | tf_op jit(solution)/shard_map/reduce_scatter | solution.py:83
  284.5 41.8 %copy-start.2 = (bf16[1024,64]{0,1:T(8,128)(2,1)S(1)}, bf16[1024,64]{0,1:T(8,128)(2,1)}, u32[]{:S(2)}) copy-start(bf16[1024,64]{0,1:T(8,128)(2,1)} %param.21) | copy-start | bytes 393220
  284.5 31.7 %all-to-all-start.5 = ((bf16[8,128,1024]{2,1,0:T(8,128)(2,1)}), bf16[8,128,1024]{2,1,0:T(8,128)(2,1)}, u32[]{:S(2)}, u32[]{:S(2)}) async-start(bf16[8,128,1024]{2,1,0:T(8,128)(2,1)} %bitcast.96), calls=%async_computation.6 | async-start | bytes 4194304 | tf_op jit(solution)/shard_map/all_to_all | solution.py:29
  316.1 24.5 %all-to-all-start.7 = ((bf16[32,2,3,1024]{3,1,2,0:T(2,128)(2,1)}), bf16[32,2,3,1024]{3,1,2,0:T(2,128)(2,1)S(1)}, u32[]{:S(2)}, u32[]{:S(2)}) async-start(bf16[32,2,3,1024]{3,1,2,0:T(2,128)(2,1)} %copy.37), calls=%async_computation.9 | async-start | bytes 786432 | tf_op jit(solution)/shard_map/all_to_all | solution.py:92
Sparse Core Ops, SparseCore 0:
  42.7 24.9 all-gather.2
  75.0 49.9 reduce-scatter.2
  206.7 24.4 all-gather.4
  239.2 50.5 reduce-scatter.4
where the time goes:
time: 355 us; the launch traced here: 354 us
  blocking collectives  125 us (35%)
  waiting for transfers between devices  124 us (35%)
  starting transfers between devices  29.5 us (8%)
  matrix products  27.8 us (8%)
  other arithmetic  18.2 us (5%)
  local copies, waits for them, and re-layouts  15.4 us (4%)
  between operations  13.4 us (4%)
    all_to_all x2, blocking collectives, from_everyone(): return lax.all_to_all(copies, axis, split_axis=0, concat_axis=0, tiled=True)  78 us
    all_gather x2, waiting for transfers between devices, moe_layer(): lax.all_gather(arrived, 'dp', axis=0, tiled=True)  49.5 us
    all_to_all x2, waiting for transfers between devices, summed_on_arrival(): lax.all_to_all(in_blocks(value, dim, devices), axis, 0, 0, tiled=True)  48.7 us
    all_to_all x2, blocking collectives, moe_layer(): lax.all_to_all(buffer, 'expert', split_axis=0, concat_axis=0, tiled=True)  47.2 us
    all_to_all x2, waiting for transfers between devices, moe_layer(): lax.all_to_all(partial_value.astype(jnp.bfloat16), 'expert', split_axis=0...  25.4 us
    all_to_all x2, starting transfers between devices, moe_layer(): lax.all_to_all(partial_value.astype(jnp.bfloat16), 'expert', split_axis=0...  20.2 us
    dot_general x2, matrix products, moe_layer(): jnp.einsum('secf,efd->secd', rows, e_out, preferred_element_type=jnp.floa...  15 us
    dot_general x2, matrix products, moe_layer(): jnp.dot(rows, d_out, preferred_element_type=jnp.float32)  12.4 us
  transfers between devices with their start and end apart: 8, of which 7 were waited for; matrix products, arithmetic and copies ran while one was open for 7% of the time, Pallas kernels for 0%

commit v1 on v0

--- a/solution.py
+++ b/solution.py
@@ -2,6 +2,20 @@
 import jax.numpy as jnp
 from jax import lax
 from jax.sharding import PartitionSpec as P
+
+
+def on_each_block(x, axis, dim, make, out_dim):
+    ways, here, step = (lax.axis_size(axis), lax.axis_index(axis), x.shape[dim])
+    earlier, later = ([], [])
+    going_up = going_down = x
+    for far in range(ways // 2 + 1):
+        earlier.append(make(going_up, (here - far) % ways * step))
+        if 0 < far < ways - ways // 2:
+            later.append(make(going_down, (here + far) % ways * step))
+        going_up = lax.ppermute(going_up, axis, [(d, (d + 1) % ways) for d in range(ways)])
+        going_down = lax.ppermute(going_down, axis, [(d, (d - 1) % ways) for d in range(ways)])
+    line = jnp.concatenate([*earlier[::-1], *later], axis=out_dim)
+    return jnp.roll(line, (here - ways // 2) * earlier[0].shape[out_dim], axis=out_dim)
 
 
 def in_order(blocks, dim):
@@ -71,11 +85,14 @@
     buffer = buffer.reshape(owners, per_dev, cap, width)
     arrived = lax.all_to_all(buffer, "expert", split_axis=0, concat_axis=0, tiled=True)
     expert_act = jax.nn.gelu(
-        jnp.einsum(
-            "secd,edf->secf",
-            lax.all_gather(arrived, "dp", axis=0, tiled=True),
-            e_in,
-            preferred_element_type=jnp.float32,
+        on_each_block(
+            arrived,
+            "dp",
+            0,
+            lambda part, offset: jnp.einsum(
+                "secd,edf->secf", part, e_in, preferred_element_type=jnp.float32
+            ),
+            0,
         ),
         approximate=True,
     ).astype(jnp.bfloat16)

time: 355 us -> 368 us (1.037)
  starting transfers between devices: 29.5 us -> 36.4 us
  blocking collectives: 125 us -> 129 us
    all_gather x2 -> x0, waiting for transfers between devices: 49.5 us -> none  [moe_layer(): lax.all_gather(arrived, 'dp', axis=0, tiled=True)]
    ppermute x0 -> x14, waiting for transfers between devices: none -> 46.9 us  [the longest x8 46.7 us: on_each_block(): lax.ppermute(going_up, axis, [(d, (d + 1) % ways) for d in range(ways)])]
    ppermute x0 -> x14, starting transfers between devices: none -> 18 us  [the longest x6 18 us: on_each_block(): lax.ppermute(going_down, axis, [(d, (d - 1) % ways) for d in range(ways)])]
    all_to_all x2, starting transfers between devices: 20.2 us -> 9.35 us  [moe_layer(): lax.all_to_all(partial_value.astype(jnp.bfloat16), 'expert', split_axis=0...]
    dot_general x0 -> x16, matrix products: none -> 10.4 us  [moe_layer(): jnp.einsum('secd,edf->secf', part, e_in, preferred_element_type=jnp.float32)]
    dot_general x2, matrix products: 15 us -> 6.95 us  [moe_layer(): jnp.einsum('secf,efd->secd', rows, e_out, preferred_element_type=jnp.floa...]
    all_to_all x2, blocking collectives: 78 us -> 82 us  [from_everyone(): return lax.all_to_all(copies, axis, split_axis=0, concat_axis=0, tiled=True)]
  transfers between devices with their start and end apart: 8 -> 20, of which waited for: 7 -> 13; matrix products, arithmetic and copies ran while one was open for 7% -> 9% of each run, Pallas kernels for 0% -> 0%
where the time goes in v1:
time: 368 us; the launch traced here: 367 us
  blocking collectives  129 us (35%)
  waiting for transfers between devices  123 us (33%)
  starting transfers between devices  36.4 us (10%)
  matrix products  30.1 us (8%)
  other arithmetic  18.3 us (5%)
  local copies, waits for them, and re-layouts  16.2 us (4%)
  between operations  14 us (4%)
    all_to_all x2, blocking collectives, from_everyone(): return lax.all_to_all(copies, axis, split_axis=0, concat_axis=0, tiled=True)  82 us
    all_to_all x2, waiting for transfers between devices, summed_on_arrival(): lax.all_to_all(in_blocks(value, dim, devices), axis, 0, 0, tiled=True)  49.5 us
    all_to_all x2, blocking collectives, moe_layer(): lax.all_to_all(buffer, 'expert', split_axis=0, concat_axis=0, tiled=True)  47.3 us
    ppermute x8, waiting for transfers between devices, on_each_block(): lax.ppermute(going_up, axis, [(d, (d + 1) % ways) for d in range(ways)])  46.7 us
    all_to_all x2, waiting for transfers between devices, moe_layer(): lax.all_to_all(partial_value.astype(jnp.bfloat16), 'expert', split_axis=0...  26.1 us
    ppermute x6, starting transfers between devices, on_each_block(): lax.ppermute(going_down, axis, [(d, (d - 1) % ways) for d in range(ways)])  18 us
    dot_general x2, matrix products, moe_layer(): jnp.dot(rows, d_out, preferred_element_type=jnp.float32)  12.4 us
    dot_general x16, matrix products, moe_layer(): jnp.einsum('secd,edf->secf', part, e_in, preferred_element_type=jnp.float32)  10.4 us
  transfers between devices with their start and end apart: 20, of which 13 were waited for; matrix products, arithmetic and copies ran while one was open for 9% of the time, Pallas kernels for 0%

profile of v1, /device:TPU:32, one launch (start us, length us, event | category | flops | bytes accessed | tf_op | source)
XLA Modules:
  0.0 366.9 jit_solution(5394407073262144370)
XLA Ops:
  10.2 1.2 fusion.111
  11.4 1.8 scatter_custom_fusion
  14.1 28.6 %all_to_all.40 = bf16[32,1,5,1024]{3,2,1,0:T(8,128)(2,1)S(1)} all-to-all(bf16[32,1,5,1024]{3,2,1,0:T(8,128)(2,1)} %bitcast.255), channel_id=1, replica_groups=mesh['dp'=8,'expert'=32] {'expert'}, dimensions={0} | all-to-all | bytes 655360 | tf_op jit(solution)/shard_map/all_to_all | solution.py:86
  42.9 7.7 %collective-permute-done = bf16[32,1,5,1024]{3,0,2,1:T(8,128)(2,1)S(1)} collective-permute-done((bf16[32,1,5,1024]{3,0,2,1:T(8,128)(2,1)S(1)}, bf16[32,1,5,1024]{3,0,2,1:T(8,128)(2,1)S(1)}, u32[]{:S(2)}, u32[]{:S(2)}) %collective-permute-start) | collective-permute-done | bytes 327712 | tf_op jit(solution)/shard_map/ppermute | solution.py:15
  50.6 3.0 collective-permute-start.4
  53.5 4.8 %collective-permute-done.1 = bf16[32,1,5,1024]{3,0,2,1:T(8,128)(2,1)S(1)} collective-permute-done((bf16[32,1,5,1024]{3,0,2,1:T(8,128)(2,1)S(1)}, bf16[32,1,5,1024]{3,0,2,1:T(8,128)(2,1)S(1)}, u32[]{:S(2)}, u32[]{:S(2)}) %collective-permute-start.1) | collective-permute-done | bytes 327712 | tf_op jit(solution)/shard_map/ppermute | solution.py:15
  58.3 3.0 collective-permute-start.5
  61.3 4.7 %collective-permute-done.2 = bf16[32,1,5,1024]{3,0,2,1:T(8,128)(2,1)} collective-permute-done((bf16[32,1,5,1024]{3,0,2,1:T(8,128)(2,1)S(1)}, bf16[32,1,5,1024]{3,0,2,1:T(8,128)(2,1)}, u32[]{:S(2)}, u32[]{:S(2)}) %collective-permute-start.2) | collective-permute-done | bytes 327712 | tf_op jit(solution)/shard_map/ppermute | solution.py:15
  66.3 3.1 collective-permute-start.6
  69.4 4.8 %collective-permute-done.3 = bf16[32,1,5,1024]{3,0,2,1:T(8,128)(2,1)} collective-permute-done((bf16[32,1,5,1024]{3,0,2,1:T(8,128)(2,1)}, bf16[32,1,5,1024]{3,0,2,1:T(8,128)(2,1)}, u32[]{:S(2)}, u32[]{:S(2)}) %collective-permute-start.3) | collective-permute-done | bytes 327712 | tf_op jit(solution)/shard_map/ppermute | solution.py:15
  74.1 1.3 constant_dynamic-update-slice_fusion.15
  75.4 1.3 constant_dynamic-update-slice_fusion.14
  77.8 1.3 constant_dynamic-update-slice_fusion.10
  79.2 1.3 constant_dynamic-update-slice_fusion.9
  81.7 3.3 convert_bitcast_fusion.1
  85.5 40.4 %all_to_all.41 = bf16[8,128,1024]{2,1,0:T(8,128)(2,1)} all-to-all(bf16[8,128,1024]{2,1,0:T(8,128)(2,1)S(1)} %broadcast_in_dim.49), channel_id=1, replica_groups=mesh['dp'=8,'expert'=32] {'dp'}, dimensions={0} | all-to-all | bytes 4194304 | tf_op jit(solution)/shard_map/all_to_all | solution.py:29
  125.9 6.2 %convolution_convert_fusion.1 = bf16[1024,1024]{1,0:T(8,128)(2,1)} fusion(bf16[512,1024]{1,0:T(8,128)(2,1)} %param.23, bf16[1024,1024]{1,0:T(8,128)(2,1)} %bitcast.253, bf16[1024,512]{1,0:T(8,128)(2,1)} %param.22), kind=kOutput, calls=%fused_computation.62 | convolution fusion | flops 2153250816 | bytes 6291456 | tf_op jit(solution)/shard_map/dot_general | solution.py:82
  132.1 4.5 %all-to-all-start.1 = ((bf16[8,128,1024]{2,1,0:T(8,128)(2,1)}), bf16[8,128,1024]{2,1,0:T(8,128)(2,1)}, u32[]{:S(2)}, u32[]{:S(2)}) async-start(bf16[8,128,1024]{2,1,0:T(8,128)(2,1)} %bitcast.251), calls=%async_computation.1 | async-start | bytes 4194304 | tf_op jit(solution)/shard_map/all_to_all | solution.py:43
  137.4 2.0 copy.44
  139.3 24.5 %all-to-all-done.1 = bf16[8,128,1024]{2,1,0:T(8,128)(2,1)} async-done(((bf16[8,128,1024]{2,1,0:T(8,128)(2,1)}), bf16[8,128,1024]{2,1,0:T(8,128)(2,1)}, u32[]{:S(2)}, u32[]{:S(2)}) %all-to-all-start.1) | async-done | bytes 2097184 | tf_op jit(solution)/shard_map/all_to_all | solution.py:43
  163.8 5.2 %all-to-all-start.3 = ((bf16[32,1,5,1024]{3,2,1,0:T(8,128)(2,1)}), bf16[32,1,5,1024]{3,2,1,0:T(8,128)(2,1)}, u32[]{:S(2)}, u32[]{:S(2)}) async-start(bf16[32,1,5,1024]{3,2,1,0:T(8,128)(2,1)} %copy.44), calls=%async_computation.4 | async-start | bytes 1048576 | tf_op jit(solution)/shard_map/all_to_all | solution.py:109
  169.1 2.8 convert_reduce_fusion.1
  171.9 14.4 %all-to-all-done.3 = bf16[32,1,5,1024]{3,2,1,0:T(8,128)(2,1)} async-done(((bf16[32,1,5,1024]{3,2,1,0:T(8,128)(2,1)}), bf16[32,1,5,1024]{3,2,1,0:T(8,128)(2,1)}, u32[]{:S(2)}, u32[]{:S(2)}) %all-to-all-start.3) | async-done | bytes 327712 | tf_op jit(solution)/shard_map/all_to_all | solution.py:109
  187.5 1.6 gather_fusion
  189.1 1.4 convert_reduce_fusion.2
  190.8 1.6 scatter_custom_fusion.1
  192.9 18.7 %all_to_all.42 = bf16[32,2,3,1024]{3,1,2,0:T(2,128)(2,1)S(1)} all-to-all(bf16[32,2,3,1024]{3,1,2,0:T(2,128)(2,1)S(1)} %copy.45), channel_id=1, replica_groups=mesh['dp'=8,'expert'=32] {'expert'}, dimensions={0} | all-to-all | bytes 786432 | tf_op jit(solution)/shard_map/all_to_all | solution.py:86
  211.8 8.4 %collective-permute-done.7 = bf16[32,2,3,1024]{3,0,2,1:T(8,128)(2,1)S(1)} collective-permute-done((bf16[32,2,3,1024]{3,0,2,1:T(8,128)(2,1)S(1)}, bf16[32,2,3,1024]{3,0,2,1:T(8,128)(2,1)S(1)}, u32[]{:S(2)}, u32[]{:S(2)}) %collective-permute-start.7) | collective-permute-done | bytes 393248 | tf_op jit(solution)/shard_map/ppermute | solution.py:15
  220.2 3.0 collective-permute-start.11
  223.1 5.5 %collective-permute-done.8 = bf16[32,2,3,1024]{3,0,2,1:T(8,128)(2,1)S(1)} collective-permute-done((bf16[32,2,3,1024]{3,0,2,1:T(8,128)(2,1)S(1)}, bf16[32,2,3,1024]{3,0,2,1:T(8,128)(2,1)S(1)}, u32[]{:S(2)}, u32[]{:S(2)}) %collective-permute-start.8) | collective-permute-done | bytes 393248 | tf_op jit(solution)/shard_map/ppermute | solution.py:15
  228.6 3.0 collective-permute-start.12
  231.5 5.5 %collective-permute-done.9 = bf16[32,2,3,1024]{3,0,2,1:T(8,128)(2,1)S(1)} collective-permute-done((bf16[32,2,3,1024]{3,0,2,1:T(8,128)(2,1)S(1)}, bf16[32,2,3,1024]{3,0,2,1:T(8,128)(2,1)S(1)}, u32[]{:S(2)}, u32[]{:S(2)}) %collective-permute-start.9) | collective-permute-done | bytes 393248 | tf_op jit(solution)/shard_map/ppermute | solution.py:15
  237.0 3.0 collective-permute-start.13
  239.9 5.5 %collective-permute-done.10 = bf16[32,2,3,1024]{3,0,2,1:T(8,128)(2,1)S(1)} collective-permute-done((bf16[32,2,3,1024]{3,0,2,1:T(8,128)(2,1)S(1)}, bf16[32,2,3,1024]{3,0,2,1:T(8,128)(2,1)S(1)}, u32[]{:S(2)}, u32[]{:S(2)}) %collective-permute-start.10) | collective-permute-done | bytes 393248 | tf_op jit(solution)/shard_map/ppermute | solution.py:15
  249.5 1.3 copy-done.13
  250.8 3.7 %convert_bitcast_fusion = bf16[256,2,3,1024]{3,0,2,1:T(8,128)(2,1)} fusion(bf16[2,512,1024]{2,1,0:T(8,128)(2,1)S(1)} %copy-done.13, f32[512,2,3,512]{3,0,2,1:T(8,128)S(1)} %constant_dynamic-update-slice_fusion.16, s32[]{:T(128)S(6)} %select_n.56), kind=kOutput, calls=%fused_computation.16 | convolution fusion | flops 1619263488 | bytes 8388612 | tf_op jit(solution)/shard_map/secf,efd->secd/dot_general | solution.py:101
  254.9 41.5 %all_to_all.43 = bf16[8,128,1024]{2,1,0:T(8,128)(2,1)} all-to-all(bf16[8,128,1024]{2,1,0:T(8,128)(2,1)S(1)} %broadcast_in_dim.54), channel_id=1, replica_groups=mesh['dp'=8,'expert'=32] {'dp'}, dimensions={0} | all-to-all | bytes 4194304 | tf_op jit(solution)/shard_map/all_to_all | solution.py:29
  296.5 6.2 %convolution_convert_fusion = bf16[1024,1024]{1,0:T(8,128)(2,1)} fusion(bf16[512,1024]{1,0:T(8,128)(2,1)} %param.25, bf16[1024,1024]{1,0:T(8,128)(2,1)} %bitcast.254, bf16[1024,512]{1,0:T(8,128)(2,1)} %param.24), kind=kOutput, calls=%fused_computation.61 | convolution fusion | flops 2153250816 | bytes 6291456 | tf_op jit(solution)/shard_map/dot_general | solution.py:82
  302.7 4.5 %all-to-all-start.5 = ((bf16[8,128,1024]{2,1,0:T(8,128)(2,1)}), bf16[8,128,1024]{2,1,0:T(8,128)(2,1)}, u32[]{:S(2)}, u32[]{:S(2)}) async-start(bf16[8,128,1024]{2,1,0:T(8,128)(2,1)} %bitcast.252), calls=%async_computation.6 | async-start | bytes 4194304 | tf_op jit(solution)/shard_map/all_to_all | solution.py:43
  307.2 2.2 copy.49
  309.3 25.0 %all-to-all-done.5 = bf16[8,128,1024]{2,1,0:T(8,128)(2,1)} async-done(((bf16[8,128,1024]{2,1,0:T(8,128)(2,1)}), bf16[8,128,1024]{2,1,0:T(8,128)(2,1)}, u32[]{:S(2)}, u32[]{:S(2)}) %all-to-all-start.5) | async-done | bytes 2097184 | tf_op jit(solution)/shard_map/all_to_all | solution.py:43
  334.3 4.2 %all-to-all-start.7 = ((bf16[32,2,3,1024]{3,1,2,0:T(2,128)(2,1)}), bf16[32,2,3,1024]{3,1,2,0:T(2,128)(2,1)S(1)}, u32[]{:S(2)}, u32[]{:S(2)}) async-start(bf16[32,2,3,1024]{3,1,2,0:T(2,128)(2,1)} %copy.49), calls=%async_computation.9 | async-start | bytes 786432 | tf_op jit(solution)/shard_map/all_to_all | solution.py:109
  338.8 2.8 convert_reduce_fusion
  341.6 11.7 %all-to-all-done.7 = bf16[32,2,3,1024]{3,1,2,0:T(2,128)(2,1)S(1)} async-done(((bf16[32,2,3,1024]{3,1,2,0:T(2,128)(2,1)}), bf16[32,2,3,1024]{3,1,2,0:T(2,128)(2,1)S(1)}, u32[]{:S(2)}, u32[]{:S(2)}) %all-to-all-start.7) | async-done | bytes 393248 | tf_op jit(solution)/shard_map/all_to_all | solution.py:109
  353.4 1.5 copy.51
  354.9 1.6 reshape.378
  356.5 1.6 gather_fusion.1
  358.1 2.0 fusion.117
  (108 shorter events, 15.2 us)
Async XLA Ops:
  6.5 238.9 %copy-start = (bf16[2,1024,512]{2,1,0:T(8,128)(2,1)S(1)}, bf16[2,1024,512]{2,1,0:T(8,128)(2,1)}, u32[]{:S(2)}) copy-start(bf16[2,1024,512]{2,1,0:T(8,128)(2,1)} %param.28) | copy-start | bytes 6291460
  6.5 67.6 %copy-start.1 = (bf16[1,1024,512]{2,1,0:T(8,128)(2,1)S(1)}, bf16[1,1024,512]{2,1,0:T(8,128)(2,1)}, u32[]{:S(2)}) copy-start(bf16[1,1024,512]{2,1,0:T(8,128)(2,1)} %param.26) | copy-start | bytes 3145732
  6.5 130.8 %reduce-scatter.3.cloned.1.call-start = ((), (), s32[]{:S(2)}) async-start(), calls=%async_computation.10 | async-start | bytes 2949120 | tf_op jit(solution)/shard_map/reduce_scatter | solution.py:100
  42.8 7.7 %collective-permute-start = (bf16[32,1,5,1024]{3,0,2,1:T(8,128)(2,1)S(1)}, bf16[32,1,5,1024]{3,0,2,1:T(8,128)(2,1)S(1)}, u32[]{:S(2)}, u32[]{:S(2)}) collective-permute-start(bf16[32,1,5,1024]{3,0,2,1:T(8,128)(2,1)S(1)} %copy.41), channel_id=1, source_target_pairs={{0,32},{32,64},{64,96},{96,128},{128,160},{160,192},{192,224},{224... | collective-permute-start | bytes 983048 | tf_op jit(solution)/shard_map/ppermute | solution.py:15
  50.6 7.7 %copy-start.3 = (bf16[32,1,5,1024]{3,0,2,1:T(8,128)(2,1)}, bf16[32,1,5,1024]{3,0,2,1:T(8,128)(2,1)S(1)}, u32[]{:S(2)}) copy-start(bf16[32,1,5,1024]{3,0,2,1:T(8,128)(2,1)S(1)} %collective-permute-done) | copy-start | bytes 983044
  50.6 7.7 %collective-permute-start.1 = (bf16[32,1,5,1024]{3,0,2,1:T(8,128)(2,1)S(1)}, bf16[32,1,5,1024]{3,0,2,1:T(8,128)(2,1)S(1)}, u32[]{:S(2)}, u32[]{:S(2)}) collective-permute-start(bf16[32,1,5,1024]{3,0,2,1:T(8,128)(2,1)S(1)} %collective-permute-done), channel_id=1, source_target_pairs={{0,32},{32,64},{64,96},{96,128},{128,160},{160,192},{192,224},{224... | collective-permute-start | bytes 983048 | tf_op jit(solution)/shard_map/ppermute | solution.py:15
  50.6 7.7 %collective-permute-start.4 = (bf16[32,1,5,1024]{3,0,2,1:T(8,128)(2,1)S(1)}, bf16[32,1,5,1024]{3,0,2,1:T(8,128)(2,1)}, u32[]{:S(2)}, u32[]{:S(2)}) collective-permute-start(bf16[32,1,5,1024]{3,0,2,1:T(8,128)(2,1)S(1)} %copy.41), channel_id=1, source_target_pairs={{0,224},{32,0},{64,32},{96,64},{128,96},{160,128},{192,160},{224,1... | collective-permute-start | bytes 983048 | tf_op jit(solution)/shard_map/ppermute | solution.py:16
  58.3 3.1 copy-start.5
  58.3 7.8 %collective-permute-start.2 = (bf16[32,1,5,1024]{3,0,2,1:T(8,128)(2,1)S(1)}, bf16[32,1,5,1024]{3,0,2,1:T(8,128)(2,1)}, u32[]{:S(2)}, u32[]{:S(2)}) collective-permute-start(bf16[32,1,5,1024]{3,0,2,1:T(8,128)(2,1)S(1)} %collective-permute-done.1), channel_id=1, source_target_pairs={{0,32},{32,64},{64,96},{96,128},{128,160},{160,192},{192,224},{224... | collective-permute-start | bytes 983048 | tf_op jit(solution)/shard_map/ppermute | solution.py:15
  58.3 8.0 %collective-permute-start.5 = (bf16[32,1,5,1024]{3,0,2,1:T(8,128)(2,1)}, bf16[32,1,5,1024]{3,0,2,1:T(8,128)(2,1)}, u32[]{:S(2)}, u32[]{:S(2)}) collective-permute-start(bf16[32,1,5,1024]{3,0,2,1:T(8,128)(2,1)} %collective-permute-done.4), channel_id=1, source_target_pairs={{0,224},{32,0},{64,32},{96,64},{128,96},{160,128},{192,160},{224,1... | collective-permute-start | bytes 983048 | tf_op jit(solution)/shard_map/ppermute | solution.py:16
  66.1 8.0 %collective-permute-start.3 = (bf16[32,1,5,1024]{3,0,2,1:T(8,128)(2,1)}, bf16[32,1,5,1024]{3,0,2,1:T(8,128)(2,1)}, u32[]{:S(2)}, u32[]{:S(2)}) collective-permute-start(bf16[32,1,5,1024]{3,0,2,1:T(8,128)(2,1)} %collective-permute-done.2), channel_id=1, source_target_pairs={{0,32},{32,64},{64,96},{96,128},{128,160},{160,192},{192,224},{224... | collective-permute-start | bytes 983048 | tf_op jit(solution)/shard_map/ppermute | solution.py:15
  66.1 10.7 %copy-start.6 = (bf16[32,1,5,1024]{3,0,2,1:T(8,128)(2,1)S(1)}, bf16[32,1,5,1024]{3,0,2,1:T(8,128)(2,1)}, u32[]{:S(2)}) copy-start(bf16[32,1,5,1024]{3,0,2,1:T(8,128)(2,1)} %copy-done.5) | copy-start | bytes 983044
  66.1 11.0 %copy-start.4 = (bf16[32,1,5,1024]{3,0,2,1:T(8,128)(2,1)S(1)}, bf16[32,1,5,1024]{3,0,2,1:T(8,128)(2,1)}, u32[]{:S(2)}) copy-start(bf16[32,1,5,1024]{3,0,2,1:T(8,128)(2,1)} %copy-done.3) | copy-start | bytes 983044
  66.3 14.2 %collective-permute-start.6 = (bf16[32,1,5,1024]{3,0,2,1:T(8,128)(2,1)}, bf16[32,1,5,1024]{3,0,2,1:T(8,128)(2,1)S(1)}, u32[]{:S(2)}, u32[]{:S(2)}) collective-permute-start(bf16[32,1,5,1024]{3,0,2,1:T(8,128)(2,1)} %collective-permute-done.5), channel_id=1, source_target_pairs={{0,224},{32,0},{64,32},{96,64},{128,96},{160,128},{192,160},{224,1... | collective-permute-start | bytes 983048 | tf_op jit(solution)/shard_map/ppermute | solution.py:16
  80.5 1.2 copy-start.14
  81.7 3.3 copy-start.2
  81.7 3.3 copy-start.9
  132.1 4.5 %copy-start.12 = (s32[128,1]{0,1:T(1,128)S(1)}, s32[128,1]{0,1:T(1,128)}, u32[]{:S(2)}) copy-start(s32[128,1]{0,1:T(1,128)} %param.17) | copy-start | bytes 1540
  132.1 5.0 %copy-start.8 = (bf16[1024,32]{0,1:T(8,128)(2,1)S(1)}, bf16[1024,32]{0,1:T(8,128)(2,1)}, u32[]{:S(2)}) copy-start(bf16[1024,32]{0,1:T(8,128)(2,1)} %param.20) | copy-start | bytes 196612
  132.1 5.0 %copy-start.11 = (s32[128,1]{0,1:T(1,128)S(1)}, s32[128,1]{0,1:T(1,128)}, u32[]{:S(2)}) copy-start(s32[128,1]{0,1:T(1,128)} %param.16) | copy-start | bytes 1540
  132.1 31.7 %all-to-all-start.1 = ((bf16[8,128,1024]{2,1,0:T(8,128)(2,1)}), bf16[8,128,1024]{2,1,0:T(8,128)(2,1)}, u32[]{:S(2)}, u32[]{:S(2)}) async-start(bf16[8,128,1024]{2,1,0:T(8,128)(2,1)} %bitcast.251), calls=%async_computation.1 | async-start | bytes 4194304 | tf_op jit(solution)/shard_map/all_to_all | solution.py:43
  163.8 22.5 %all-to-all-start.3 = ((bf16[32,1,5,1024]{3,2,1,0:T(8,128)(2,1)}), bf16[32,1,5,1024]{3,2,1,0:T(8,128)(2,1)}, u32[]{:S(2)}, u32[]{:S(2)}) async-start(bf16[32,1,5,1024]{3,2,1,0:T(8,128)(2,1)} %copy.44), calls=%async_computation.4 | async-start | bytes 1048576 | tf_op jit(solution)/shard_map/all_to_all | solution.py:109
  169.0 138.2 %reduce-scatter.5.cloned.1.call-start = ((), (), s32[]{:S(2)}) async-start(), calls=%async_computation.11 | async-start | bytes 3538944 | tf_op jit(solution)/shard_map/reduce_scatter | solution.py:100
  187.5 3.3 copy-start.10
  211.7 8.4 %collective-permute-start.7 = (bf16[32,2,3,1024]{3,0,2,1:T(8,128)(2,1)S(1)}, bf16[32,2,3,1024]{3,0,2,1:T(8,128)(2,1)S(1)}, u32[]{:S(2)}, u32[]{:S(2)}) collective-permute-start(bf16[32,2,3,1024]{3,0,2,1:T(8,128)(2,1)S(1)} %copy.46), channel_id=1, source_target_pairs={{0,32},{32,64},{64,96},{96,128},{128,160},{160,192},{192,224},{224... | collective-permute-start | bytes 1179656 | tf_op jit(solution)/shard_map/ppermute | solution.py:15
  220.2 8.4 %collective-permute-start.8 = (bf16[32,2,3,1024]{3,0,2,1:T(8,128)(2,1)S(1)}, bf16[32,2,3,1024]{3,0,2,1:T(8,128)(2,1)S(1)}, u32[]{:S(2)}, u32[]{:S(2)}) collective-permute-start(bf16[32,2,3,1024]{3,0,2,1:T(8,128)(2,1)S(1)} %collective-permute-done.7), channel_id=1, source_target_pairs={{0,32},{32,64},{64,96},{96,128},{128,160},{160,192},{192,224},{224... | collective-permute-start | bytes 1179656 | tf_op jit(solution)/shard_map/ppermute | solution.py:15
  220.2 8.4 %collective-permute-start.11 = (bf16[32,2,3,1024]{3,0,2,1:T(8,128)(2,1)S(1)}, bf16[32,2,3,1024]{3,0,2,1:T(8,128)(2,1)S(1)}, u32[]{:S(2)}, u32[]{:S(2)}) collective-permute-start(bf16[32,2,3,1024]{3,0,2,1:T(8,128)(2,1)S(1)} %copy.46), channel_id=1, source_target_pairs={{0,224},{32,0},{64,32},{96,64},{128,96},{160,128},{192,160},{224,1... | collective-permute-start | bytes 1179656 | tf_op jit(solution)/shard_map/ppermute | solution.py:16
  228.6 8.4 %collective-permute-start.9 = (bf16[32,2,3,1024]{3,0,2,1:T(8,128)(2,1)S(1)}, bf16[32,2,3,1024]{3,0,2,1:T(8,128)(2,1)S(1)}, u32[]{:S(2)}, u32[]{:S(2)}) collective-permute-start(bf16[32,2,3,1024]{3,0,2,1:T(8,128)(2,1)S(1)} %collective-permute-done.8), channel_id=1, source_target_pairs={{0,32},{32,64},{64,96},{96,128},{128,160},{160,192},{192,224},{224... | collective-permute-start | bytes 1179656 | tf_op jit(solution)/shard_map/ppermute | solution.py:15
  228.6 8.4 %collective-permute-start.12 = (bf16[32,2,3,1024]{3,0,2,1:T(8,128)(2,1)S(1)}, bf16[32,2,3,1024]{3,0,2,1:T(8,128)(2,1)S(1)}, u32[]{:S(2)}, u32[]{:S(2)}) collective-permute-start(bf16[32,2,3,1024]{3,0,2,1:T(8,128)(2,1)S(1)} %collective-permute-done.11), channel_id=1, source_target_pairs={{0,224},{32,0},{64,32},{96,64},{128,96},{160,128},{192,160},{224,1... | collective-permute-start | bytes 1179656 | tf_op jit(solution)/shard_map/ppermute | solution.py:16
  237.0 8.4 %collective-permute-start.10 = (bf16[32,2,3,1024]{3,0,2,1:T(8,128)(2,1)S(1)}, bf16[32,2,3,1024]{3,0,2,1:T(8,128)(2,1)S(1)}, u32[]{:S(2)}, u32[]{:S(2)}) collective-permute-start(bf16[32,2,3,1024]{3,0,2,1:T(8,128)(2,1)S(1)} %collective-permute-done.9), channel_id=1, source_target_pairs={{0,32},{32,64},{64,96},{96,128},{128,160},{160,192},{192,224},{224... | collective-permute-start | bytes 1179656 | tf_op jit(solution)/shard_map/ppermute | solution.py:15
  237.0 11.7 %collective-permute-start.13 = (bf16[32,2,3,1024]{3,0,2,1:T(8,128)(2,1)S(1)}, bf16[32,2,3,1024]{3,0,2,1:T(8,128)(2,1)S(1)}, u32[]{:S(2)}, u32[]{:S(2)}) collective-permute-start(bf16[32,2,3,1024]{3,0,2,1:T(8,128)(2,1)S(1)} %collective-permute-done.12), channel_id=1, source_target_pairs={{0,224},{32,0},{64,32},{96,64},{128,96},{160,128},{192,160},{224,1... | collective-permute-start | bytes 1179656 | tf_op jit(solution)/shard_map/ppermute | solution.py:16
  249.2 1.6 copy-start.13
  302.6 35.9 %copy-start.7 = (bf16[1024,64]{0,1:T(8,128)(2,1)S(1)}, bf16[1024,64]{0,1:T(8,128)(2,1)}, u32[]{:S(2)}) copy-start(bf16[1024,64]{0,1:T(8,128)(2,1)} %param.21) | copy-start | bytes 393220
  302.7 31.7 %all-to-all-start.5 = ((bf16[8,128,1024]{2,1,0:T(8,128)(2,1)}), bf16[8,128,1024]{2,1,0:T(8,128)(2,1)}, u32[]{:S(2)}, u32[]{:S(2)}) async-start(bf16[8,128,1024]{2,1,0:T(8,128)(2,1)} %bitcast.252), calls=%async_computation.6 | async-start | bytes 4194304 | tf_op jit(solution)/shard_map/all_to_all | solution.py:43
  334.3 19.0 %all-to-all-start.7 = ((bf16[32,2,3,1024]{3,1,2,0:T(2,128)(2,1)}), bf16[32,2,3,1024]{3,1,2,0:T(2,128)(2,1)S(1)}, u32[]{:S(2)}, u32[]{:S(2)}) async-start(bf16[32,2,3,1024]{3,1,2,0:T(2,128)(2,1)} %copy.49), calls=%async_computation.9 | async-start | bytes 786432 | tf_op jit(solution)/shard_map/all_to_all | solution.py:109
Sparse Core Ops, SparseCore 0:
  85.1 47.5 reduce-scatter.2
  254.6 50.2 reduce-scatter.4
